TPU v7x, 128 devices: a whole 4x4x4 slice. The times are simulated.
128 devices in a mesh: seq: 8 (over x, core), tp: 16 (over y, z).
Axes of the slice: x: 4, y: 4, z: 4, core: 2. Of those that a mesh axis runs over, the one named last changes fastest.
Arguments:
- vit_input: bfloat16 [8192, 1280], P(('seq', 'tp')), may hold values from -6 to 6
- image_lengths: int32 [8, 2], P('seq'), may hold values from 1 to 192, 256 in all within a row
- positions: int32 [2048], replicated, may hold values from 0 to 2047, each once
- vit_ln_gain: float32 [1280], replicated, may hold values from 0.25 to 1.75
- w_qkv: bfloat16 [1280, 3, 1280], P(None, None, 'tp'), may hold values from -0.15625 to 0.15625
- w_proj: bfloat16 [1280, 1280], P('tp'), may hold values from -0.15625 to 0.15625
- merger_ln_gain: float32 [1280], replicated, may hold values from 0.25 to 1.75
- merger_w1: bfloat16 [5120, 5120], P(None, 'tp'), may hold values from -0.078125 to 0.078125
- merger_w2: bfloat16 [5120, 8192], P('tp'), may hold values from -0.36336105 to 0.36336105
- norm_gain: float32 [8192], P('seq'), may hold values from 0.25 to 1.75
- gate_up_weight: bfloat16 [8192, 2, 29568], P('seq', None, 'tp'), may hold values from -0.0625 to 0.0625
- down_weight: bfloat16 [29568, 8192], P('tp', 'seq'), may hold values from -0.125 to 0.125
Outputs:
- mixed: bfloat16 [2048, 8192], P('tp', 'seq')
Inputs may be any that keep to these rules, and one draw needn't show every extreme that they name: `image_lengths`: each row sums to 256. `positions`: a permutation: every slot once.
All inputs are finite; a program needn't handle non-finite values.
Results may differ from a plain program's by a relative error of at most 0.038.
Values may be sent and summed in bfloat16 or wider, within the bound.
A program may use at most 128 MiB of HBM per device.

v0:
```python
import jax
import jax.numpy as jnp
from jax import lax
from jax.sharding import Mesh
from jax.sharding import PartitionSpec as P

D = 8192
HD = 80
TP = ("tp_0", "tp_1")
SEQ_TP = ("seq", "tp_0", "tp_1")


def from_everyone(x, axis):
    copies = jnp.broadcast_to(x, (lax.axis_size(axis), *x.shape))
    return lax.all_to_all(copies, axis, split_axis=0, concat_axis=0, tiled=True)


def laid_out(tiles, dim):
    shape = list(tiles.shape[1:])
    shape[dim] *= tiles.shape[0]
    return jnp.moveaxis(tiles, 0, dim).reshape(shape)


def gathered_copies(x, axis, dim):
    tiles = from_everyone(x, axis)
    return laid_out(tiles, dim)


def cut_along(x, dim, devices):
    before, after = (x.shape[:dim], x.shape[dim + 1 :])
    return jnp.moveaxis(x.reshape(*before, devices, -1, *after), dim, 0)


def sum_at_owner(x, axis, dim):
    devices = lax.axis_size(axis)
    tiles = lax.all_to_all(cut_along(x, dim, devices), axis, 0, 0, tiled=True)
    return jnp.sum(tiles.astype(jnp.float32), axis=0)


def over_copies(x, axis):
    everything = from_everyone(x, axis)
    return jnp.sum(everything, axis=0)


def sum_by_axis(x, axes, dim):
    if not axes:
        return x
    nearer = lax.psum_scatter(x, axes[0], scatter_dimension=dim, tiled=True)
    return sum_by_axis(nearer, axes[1:], dim)


def layer_norm(values, gain):
    mean = jnp.mean(values, axis=-1, keepdims=True)
    centered = values - mean
    variance = jnp.mean(centered * centered, axis=-1, keepdims=True)
    return centered * lax.rsqrt(variance + 1e-06) * gain


def image_ids(lengths, count):
    image_ends = jnp.cumsum(lengths) * 4
    patch_index = jnp.arange(count, dtype=jnp.int32)
    return jnp.sum((patch_index[:, None] >= image_ends[None, :]).astype(jnp.int32), axis=1)


def attend(query, keys, values, image_index):
    scores = jnp.einsum("qhe,khe->hqk", query, keys, preferred_element_type=jnp.float32) * HD ** (
        -0.5
    )
    same_image = image_index[:, None] == image_index[None, :]
    scores = jnp.where(same_image[None], scores, -1e30)
    top = jnp.max(scores, axis=-1, keepdims=True)
    expo = jnp.exp(scores - top)
    weights = (expo / jnp.sum(expo, axis=-1, keepdims=True)).astype(jnp.bfloat16)
    output = jnp.einsum("hqk,khe->qhe", weights, values, preferred_element_type=jnp.float32)
    return output.astype(jnp.bfloat16)


def slot_sources(positions):
    count = positions.shape[0]
    return jnp.zeros((count,), jnp.int32).at[positions].set(jnp.arange(count, dtype=jnp.int32))


def local(
    vit_input,
    image_lengths,
    positions,
    vit_ln_gain,
    w_qkv,
    w_proj,
    merger_ln_gain,
    merger_w1,
    merger_w2,
    norm_gain,
    gate_up_weight,
    down_weight,
):
    tp_size = lax.axis_size(TP)
    seq_size = lax.axis_size("seq")
    own_patches = vit_input.shape[0]
    patch_width = vit_input.shape[1]
    head_cols = w_qkv.shape[2]
    local_heads = head_cols // HD
    normed_patches = layer_norm(vit_input.astype(jnp.float32), vit_ln_gain).astype(jnp.bfloat16)
    w_qkv_flat = w_qkv.reshape(patch_width, 3 * head_cols)
    projected = jnp.dot(
        gathered_copies(normed_patches, TP, 0), w_qkv_flat, preferred_element_type=jnp.float32
    ).astype(jnp.bfloat16)
    group_patches = projected.shape[0]
    projected = projected.reshape(group_patches, 3, local_heads, HD)
    image_index = image_ids(image_lengths[0], group_patches)
    attended = attend(projected[:, 0], projected[:, 1], projected[:, 2], image_index).reshape(
        group_patches, head_cols
    )
    picked = attended
    attn_sum = sum_at_owner(
        jnp.dot(picked, w_proj, preferred_element_type=jnp.float32).astype(jnp.bfloat16), TP, 0
    )
    vit_out = vit_input.astype(jnp.float32) + attn_sum
    own_tokens = own_patches // 4
    merged_in = (
        layer_norm(vit_out, merger_ln_gain)
        .astype(jnp.bfloat16)
        .reshape(own_tokens, 4 * patch_width)
    )
    expanded = jax.nn.gelu(
        jnp.dot(gathered_copies(merged_in, TP, 0), merger_w1, preferred_element_type=jnp.float32),
        approximate=False,
    ).astype(jnp.bfloat16)
    picked = expanded
    vis_rows = sum_at_owner(
        jnp.dot(picked, merger_w2, preferred_element_type=jnp.float32).astype(jnp.bfloat16), TP, 0
    ).astype(jnp.bfloat16)
    blocks = lax.all_to_all(vis_rows, "seq", split_axis=1, concat_axis=0, tiled=True)
    gathered = lax.all_gather(blocks, TP, axis=0, tiled=True)
    col_width = gathered.shape[1]
    all_tokens = (
        gathered.reshape(tp_size, seq_size, own_tokens, col_width)
        .transpose(1, 0, 2, 3)
        .reshape(tp_size * seq_size * own_tokens, col_width)
    )
    seq_rows = all_tokens.shape[0]
    seq_tokens = jnp.take(all_tokens, slot_sources(positions), axis=0)
    token_values = seq_tokens.astype(jnp.float32)
    row_squares = over_copies(jnp.sum(token_values * token_values, axis=1), "seq")
    inverse_rms = lax.rsqrt(row_squares / D + 1e-06)
    normed = (token_values * inverse_rms[:, None] * norm_gain).astype(jnp.bfloat16)
    slice_width = seq_tokens.shape[1]
    hidden_width = gate_up_weight.shape[2]
    weight_flat = gate_up_weight.reshape(slice_width, 2 * hidden_width)
    out_rows = seq_rows // tp_size
    picked = normed
    gate_up = lax.psum_scatter(
        jnp.dot(picked, weight_flat, preferred_element_type=jnp.float32).astype(jnp.bfloat16),
        "seq",
        scatter_dimension=0,
        tiled=True,
    ).astype(jnp.float32)
    hidden = (jax.nn.silu(gate_up[:, :hidden_width]) * gate_up[:, hidden_width:]).astype(
        jnp.bfloat16
    )
    terms = jnp.dot(
        lax.all_gather(hidden, "seq", axis=0, tiled=True),
        down_weight,
        preferred_element_type=jnp.float32,
    )
    down_sum = sum_by_axis(terms.astype(jnp.bfloat16), TP, 0).astype(jnp.float32)
    residual = lax.dynamic_slice_in_dim(token_values, lax.axis_index(TP) * out_rows, out_rows, 0)
    return (residual + down_sum).astype(jnp.bfloat16)


def solution(mesh):
    finer = Mesh(mesh.devices.reshape(mesh.shape["seq"], 4, 4), ("seq", "tp_0", "tp_1"))
    in_specs = (
        P(SEQ_TP, None),
        P("seq", None),
        P(),
        P(),
        P(None, None, TP),
        P(TP, None),
        P(),
        P(None, TP),
        P(TP, None),
        P("seq"),
        P("seq", None, TP),
        P(TP, "seq"),
    )
    out_specs = P(TP, "seq")
    return jax.shard_map(local, mesh=finer, in_specs=in_specs, out_specs=out_specs, check_vma=False)
```

profile of v0, /device:TPU:0, one launch (start us, length us, event | category | flops | bytes accessed | tf_op | source)
XLA Modules:
  0.0 555.1 jit_solution(18318716780304703547)
XLA Ops:
  6.5 1.2 convert_reduce_fusion.1
  7.7 1.1 fusion.11
  8.9 1.0 fusion.13
  9.9 1.8 broadcast_in_dim.26
  11.7 8.2 %all-to-all-start = ((bf16[16,64,1280]{2,1,0:T(8,128)(2,1)}), bf16[16,64,1280]{2,1,0:T(8,128)(2,1)}, u32[]{:S(2)}, u32[]{:S(2)}) async-start(bf16[16,64,1280]{2,1,0:T(8,128)(2,1)} %broadcast_in_dim.26), calls=%async_computation | async-start | bytes 5242880 | tf_op jit(solution)/shard_map/all_to_all | solution.py:15
  19.9 0.0 all-gather.3.cloned.1.call-start
  20.0 0.2 reduce-window.8
  20.2 0.1 fusion.57
  20.3 36.8 %all-to-all-done = bf16[16,64,1280]{2,1,0:T(8,128)(2,1)} async-done(((bf16[16,64,1280]{2,1,0:T(8,128)(2,1)}), bf16[16,64,1280]{2,1,0:T(8,128)(2,1)}, u32[]{:S(2)}, u32[]{:S(2)}) %all-to-all-start) | async-done | bytes 2621472 | tf_op jit(solution)/shard_map/all_to_all | solution.py:15
  57.1 2.7 convolution_convert_fusion.4
  59.8 0.9 fusion.4
  60.7 1.9 copy-done.3
  62.6 1.0 fusion.3
  63.6 6.0 %convolution_convert_fusion.2 = bf16[1024,1280]{1,0:T(8,128)(2,1)} fusion(bf16[80,1280]{1,0:T(8,128)(2,1)S(1)} %copy-done.6, f32[1024,1024]{0,1:T(8,128)} %copy-done.3, f32[1024]{0:T(1024)S(1)} %fusion.3, f32[1024]{0:T(1024)S(1)} %get-tuple-element.5, s32[1024]{0:T(1024)S(1)} %fusion.57, bf16[1024,3,1,80]{0,3,1,2:T(8,128)(2,1)} %bitcast.64), kind=kOutput, calls=%fused_computation.14 | convolution fusion | flops 385171456 | bytes 7200768 | tf_op jit(solution)/shard_map/dot_general | solution.py:116
  69.6 37.0 %all_to_all.45 = bf16[16,64,1280]{2,1,0:T(8,128)(2,1)S(1)} all-to-all(bf16[16,64,1280]{2,1,0:T(8,128)(2,1)} %bitcast.55), channel_id=1, replica_groups=mesh['seq'=8,'tp_0'=4,'tp_1'=4] {'tp_0','tp_1'}, dimensions={0} | all-to-all | bytes 5242880 | tf_op jit(solution)/shard_map/all_to_all | solution.py:36
  106.6 0.4 convert_reduce_fusion
  107.0 0.1 fusion.56
  107.1 0.2 multiply_reduce_fusion.1
  107.4 0.1 multiply_convert_fusion.2
  107.5 0.8 reshape.148
  108.3 1.2 broadcast_in_dim.47
  109.5 35.3 %all_to_all.46 = bf16[16,16,5120]{2,1,0:T(8,128)(2,1)} all-to-all(bf16[16,16,5120]{2,1,0:T(8,128)(2,1)S(1)} %broadcast_in_dim.47), channel_id=1, replica_groups=mesh['seq'=8,'tp_0'=4,'tp_1'=4] {'tp_0','tp_1'}, dimensions={0} | all-to-all | bytes 5242880 | tf_op jit(solution)/shard_map/all_to_all | solution.py:15
  144.8 10.9 %convolution_convert_fusion.1 = bf16[256,8192]{1,0:T(8,128)(2,1)} fusion(bf16[320,8192]{1,0:T(8,128)(2,1)} %param.20, bf16[256,5120]{1,0:T(8,128)(2,1)} %bitcast.56, bf16[5120,320]{0,1:T(8,128)(2,1)S(1)} %copy-done), kind=kOutput, calls=%fused_computation.3 | convolution fusion | flops 2188460032 | bytes 15335424 | tf_op jit(solution)/shard_map/dot_general | solution.py:131
  155.7 51.6 %all_to_all.47 = bf16[16,16,8192]{2,1,0:T(8,128)(2,1)} all-to-all(bf16[16,16,8192]{2,1,0:T(8,128)(2,1)} %bitcast.54), channel_id=1, replica_groups=mesh['seq'=8,'tp_0'=4,'tp_1'=4] {'tp_0','tp_1'}, dimensions={0} | all-to-all | bytes 8388608 | tf_op jit(solution)/shard_map/all_to_all | solution.py:36
  207.3 2.9 reduce_sum.100
  210.2 11.7 %all_to_all.48 = bf16[16,8,1024]{2,0,1:T(8,128)(2,1)} all-to-all(bf16[16,8,1024]{2,0,1:T(8,128)(2,1)S(1)} %bitcast.59), channel_id=1, replica_groups=mesh['seq'=8,'tp_0'=4,'tp_1'=4] {'seq'}, dimensions={1} | all-to-all | bytes 524288 | tf_op jit(solution)/shard_map/all_to_all | solution.py:133
  221.9 0.0 all-gather.3.cloned.1.call-update
  222.0 0.0 reduce-scatter.4.cloned.1.call-start
  222.0 8.0 %scatter_custom_fusion = s32[2048]{0:T(1024)S(1)} fusion(s32[2048]{0:T(1024)S(1)} %compare_select_fusion.1, s32[2048]{0:T(1024)S(1)} %iota.7, s32[]{:T(128)} %constant.45.clone.1), kind=kCustom, calls=%fused_computation.97 | custom fusion | bytes 8196 | tf_op jit(solution)/shard_map/scatter | solution.py:80
  230.1 39.4 %all-gather.3.cloned.1.call-done = bf16[2048,1024]{1,0:T(8,128)(2,1)} async-done(((bf16[128,1024]{1,0:T(8,128)(2,1)}), bf16[2048,1024]{1,0:T(8,128)(2,1)}) %all-gather.3.cloned.1.call-update) | async-done | bytes 4194320 | tf_op jit(solution)/shard_map/all_gather | solution.py:134
  269.6 5.0 copy.21
  274.6 13.7 %gather_fusion = bf16[2048,1024]{1,0:T(8,128)(2,1)} fusion(bf16[2048,1024]{1,0:T(8,128)(2,1)} %bitcast.52, s32[2048]{0:T(1024)S(1)} %fusion.58), kind=kCustom, calls=%fused_computation | custom fusion | bytes 8396800 | tf_op jit(solution)/shard_map/jit(_take)/gather | solution.py:142
  288.2 3.1 multiply_reduce_fusion
  291.4 9.7 %all_to_all.49 = f32[8,1,2048]{2,1,0:T(1,128)S(1)} all-to-all(f32[8,1,2048]{2,1,0:T(1,128)S(1)} %broadcast_in_dim.50), channel_id=1, replica_groups=mesh['seq'=8,'tp_0'=4,'tp_1'=4] {'seq'}, dimensions={0} | all-to-all | bytes 131072 | tf_op jit(solution)/shard_map/all_to_all | solution.py:15
  301.1 0.1 reduce_sum.102
  301.1 22.3 %convolution_convert_fusion = bf16[2048,3696]{0,1:T(8,128)(2,1)} fusion(bf16[1024,3696]{0,1:T(8,128)(2,1)} %bitcast.60, f32[1024]{0:T(1024)S(1)} %copy-done.7, f32[2048]{0:T(1024)S(1)} %add_rsqrt_fusion, bf16[2048,1024]{1,0:T(8,128)(2,1)} %gather_fusion, pred[2048]{0:T(1024)(128)(4,1)S(1)} %compare_and_fusion), kind=kOutput, calls=%fused_computation.2 | convolution fusion | flops 15520202752 | bytes 26916864 | tf_op jit(solution)/shard_map/dot_general | solution.py:153
  323.5 0.0 all-gather.5.cloned.1.call-start
  323.5 82.4 %reduce-scatter.4.cloned.1.call-done = bf16[256,3696]{0,1:T(8,128)(2,1)} async-done(((bf16[2048,3696]{0,1:T(8,128)(2,1)}), bf16[256,3696]{0,1:T(8,128)(2,1)}) %reduce-scatter.4.cloned.1.call-update) | async-done | bytes 1892368 | tf_op jit(solution)/shard_map/reduce_scatter | solution.py:152
  405.9 1.8 convert_element_type.83
  407.7 1.6 fusion.6
  409.3 0.0 reduce-scatter.6.cloned.1.call-start
  409.4 49.6 %all-gather.5.cloned.1.call-done = bf16[2048,1848]{0,1:T(8,128)(2,1)} async-done(((bf16[256,1848]{0,1:T(8,128)(2,1)}), bf16[2048,1848]{0,1:T(8,128)(2,1)}) %all-gather.5.cloned.1.call-update) | async-done | bytes 7569424 | tf_op jit(solution)/shard_map/all_gather | solution.py:162
  459.0 13.7 %convolution_convert_fusion.3 = bf16[2048,1024]{1,0:T(8,128)(2,1)} fusion(bf16[2048,1848]{0,1:T(8,128)(2,1)} %all-gather.5.cloned.1.call-done, bf16[1848,1024]{1,0:T(8,128)(2,1)} %param.23), kind=kOutput, calls=%fused_computation.15 | convolution fusion | flops 7753170944 | bytes 15548416 | tf_op jit(solution)/shard_map/dot_general | solution.py:161
  472.7 0.0 reduce-scatter.8.cloned.1.call-start
  472.8 47.9 %reduce-scatter.6.cloned.1.call-done = bf16[512,1024]{1,0:T(8,128)(2,1)} async-done(((bf16[2048,1024]{1,0:T(8,128)(2,1)}), bf16[512,1024]{1,0:T(8,128)(2,1)}) %reduce-scatter.6.cloned.1.call-update) | async-done | bytes 1048592 | tf_op jit(solution)/shard_map/reduce_scatter | solution.py:48
  520.8 5.3 fusion.95
  526.1 20.6 %reduce-scatter.8.cloned.1.call-done = bf16[128,1024]{1,0:T(8,128)(2,1)} async-done(((bf16[512,1024]{1,0:T(8,128)(2,1)}), bf16[128,1024]{1,0:T(8,128)(2,1)}) %reduce-scatter.8.cloned.1.call-update) | async-done | bytes 262160 | tf_op jit(solution)/shard_map/reduce_scatter | solution.py:48
  546.7 1.9 add_convert_fusion
  (35 shorter events, 0.2 us)
Async XLA Ops:
  6.5 138.2 %copy-start = (bf16[5120,320]{0,1:T(8,128)(2,1)S(1)}, bf16[5120,320]{0,1:T(8,128)(2,1)}, u32[]{:S(2)}) copy-start(bf16[5120,320]{0,1:T(8,128)(2,1)} %param.19) | copy-start | bytes 9830404
  8.9 11.1 %copy-start.8 = (s32[1,2]{1,0:T(1,128)S(1)}, s32[1,2]{1,0:T(1,128)}, u32[]{:S(2)}) copy-start(s32[1,2]{1,0:T(1,128)} %param.13) | copy-start | bytes 28
  11.7 45.3 %all-to-all-start = ((bf16[16,64,1280]{2,1,0:T(8,128)(2,1)}), bf16[16,64,1280]{2,1,0:T(8,128)(2,1)}, u32[]{:S(2)}, u32[]{:S(2)}) async-start(bf16[16,64,1280]{2,1,0:T(8,128)(2,1)} %broadcast_in_dim.26), calls=%async_computation | async-start | bytes 5242880 | tf_op jit(solution)/shard_map/all_to_all | solution.py:15
  19.9 249.6 %all-gather.3.cloned.1.call-start = ((), (), s32[]{:S(2)}) async-start(), calls=%async_computation.9 | async-start | bytes 4456448 | tf_op jit(solution)/shard_map/all_gather | solution.py:134
  59.8 0.9 copy-start.9
  59.8 3.8 copy-start.6
  60.7 1.9 copy-start.3
  69.6 37.4 %copy-start.2 = (bf16[64,1280]{1,0:T(8,128)(2,1)S(1)}, bf16[64,1280]{1,0:T(8,128)(2,1)}, u32[]{:S(2)}) copy-start(bf16[64,1280]{1,0:T(8,128)(2,1)} %param.12) | copy-start | bytes 491524
  69.6 37.7 %copy-start.5 = (f32[1280]{0:T(1024)S(1)}, f32[1280]{0:T(1024)}, u32[]{:S(2)}) copy-start(f32[1280]{0:T(1024)} %param.18) | copy-start | bytes 15364
  207.3 14.7 %copy-start.4 = (s32[2048]{0:T(1024)S(1)}, s32[2048]{0:T(1024)}, u32[]{:S(2)}) copy-start(s32[2048]{0:T(1024)} %param.14) | copy-start | bytes 24580
  222.0 184.0 %reduce-scatter.4.cloned.1.call-start = ((), (), s32[]{:S(2)}) async-start(), calls=%async_computation.10 | async-start | bytes 17031168 | tf_op jit(solution)/shard_map/reduce_scatter | solution.py:152
  288.2 12.9 %copy-start.7 = (f32[1024]{0:T(1024)S(1)}, f32[1024]{0:T(1024)}, u32[]{:S(2)}) copy-start(f32[1024]{0:T(1024)} %param.21) | copy-start | bytes 12292
  323.5 135.5 %all-gather.5.cloned.1.call-start = ((), (), s32[]{:S(2)}) async-start(), calls=%async_computation.11 | async-start | bytes 8515584 | tf_op jit(solution)/shard_map/all_gather | solution.py:162
  409.3 111.4 %reduce-scatter.6.cloned.1.call-start = ((), (), s32[]{:S(2)}) async-start(), calls=%async_computation.12 | async-start | bytes 5242880 | tf_op jit(solution)/shard_map/reduce_scatter | solution.py:48
  472.7 74.0 %reduce-scatter.8.cloned.1.call-start = ((), (), s32[]{:S(2)}) async-start(), calls=%async_computation.13 | async-start | bytes 1310720 | tf_op jit(solution)/shard_map/reduce_scatter | solution.py:48
  520.7 27.8 %copy-start.1 = (bf16[5120,320]{0,1:T(8,128)(2,1)S(1)}, bf16[5120,320]{0,1:T(8,128)(2,1)}, u32[]{:S(2)}) copy-start(bf16[5120,320]{0,1:T(8,128)(2,1)} %param.19) | copy-start | bytes 9830404
Sparse Core Ops, SparseCore 0:
  222.1 47.4 all-gather.2
  323.6 82.2 reduce-scatter.3
  409.4 49.4 all-gather.4
  472.9 47.8 reduce-scatter.5
  523.0 23.6 reduce-scatter.7
where the time goes:
time: 556 us; the launch traced here: 555 us
  waiting for transfers between devices  277 us (50%)
  blocking collectives  145 us (26%)
  matrix products  56.6 us (10%)
  local copies, waits for them, and re-layouts  32.5 us (6%)
  other arithmetic  22.1 us (4%)
  between operations  13.4 us (2%)
  starting transfers between devices  8.41 us (2%)
    all_to_all x2, blocking collectives, sum_at_owner(): tiles = lax.all_to_all(cut_along(x, dim, devices), axis, 0, 0, tiled=True)  88.6 us
    reduce_scatter x1, waiting for transfers between devices, local(): lax.psum_scatter(jnp.dot(picked, weight_flat, preferred_element_type=jnp....  82.4 us
    reduce_scatter x2, waiting for transfers between devices, sum_by_axis(): nearer = lax.psum_scatter(x, axes[0], scatter_dimension=dim, tiled=True)  68.6 us
    all_gather x1, waiting for transfers between devices, local(): lax.all_gather(hidden, 'seq', axis=0, tiled=True)  49.6 us
    all_to_all x2, blocking collectives, from_everyone(): return lax.all_to_all(copies, axis, split_axis=0, concat_axis=0, tiled=True)  45 us
    all_gather x1, waiting for transfers between devices, local(): gathered = lax.all_gather(blocks, TP, axis=0, tiled=True)  39.4 us
    all_to_all x1, waiting for transfers between devices, from_everyone(): return lax.all_to_all(copies, axis, split_axis=0, concat_axis=0, tiled=True)  36.8 us
    dot_general x1, matrix products, local(): jnp.dot(picked, weight_flat, preferred_element_type=jnp.float32)  22.3 us
  transfers between devices with their start and end apart: 6, of which 6 were waited for; matrix products, arithmetic and copies ran while one was open for 2% of the time, Pallas kernels for 0%

commit v1 on v0

--- a/solution.py
+++ b/solution.py
@@ -1,3 +1,4 @@
+import functools
 import jax
 import jax.numpy as jnp
 from jax import lax
@@ -8,6 +9,18 @@
 HD = 80
 TP = ("tp_0", "tp_1")
 SEQ_TP = ("seq", "tp_0", "tp_1")
+
+
+def track_windows(z_in, group_axis):
+    return jnp.concatenate(
+        lax.all_to_all(
+            jnp.stack([z_in for _ in range(lax.axis_size(group_axis))], axis=0), group_axis, 0, 0
+        ),
+        0,
+    )
+
+
+use_pairs_all_by_axis = functools.partial(track_windows, group_axis="seq")
 
 
 def from_everyone(x, axis):
@@ -158,11 +171,7 @@
     hidden = (jax.nn.silu(gate_up[:, :hidden_width]) * gate_up[:, hidden_width:]).astype(
         jnp.bfloat16
     )
-    terms = jnp.dot(
-        lax.all_gather(hidden, "seq", axis=0, tiled=True),
-        down_weight,
-        preferred_element_type=jnp.float32,
-    )
+    terms = jnp.dot(use_pairs_all_by_axis(hidden), down_weight, preferred_element_type=jnp.float32)
     down_sum = sum_by_axis(terms.astype(jnp.bfloat16), TP, 0).astype(jnp.float32)
     residual = lax.dynamic_slice_in_dim(token_values, lax.axis_index(TP) * out_rows, out_rows, 0)
     return (residual + down_sum).astype(jnp.bfloat16)

time: 556 us -> 597 us (1.074)
  blocking collectives: 145 us -> 234 us
  waiting for transfers between devices: 277 us -> 226 us
    all_to_all x0 -> x1, blocking collectives: none -> 88.4 us  [track_windows(): lax.all_to_all(jnp.stack([z_in for _ in range(lax.axis_size(group_axis))]...]
    all_gather x1 -> x0, waiting for transfers between devices: 49.6 us -> none  [local(): lax.all_gather(hidden, 'seq', axis=0, tiled=True)]
  transfers between devices with their start and end apart: 6 -> 5, of which waited for: 6 -> 5; matrix products, arithmetic and copies ran while one was open for 2% -> 2% of each run, Pallas kernels for 0% -> 0%
where the time goes in v1:
time: 597 us; the launch traced here: 596 us
  blocking collectives  234 us (39%)
  waiting for transfers between devices  226 us (38%)
  matrix products  56.5 us (9%)
  local copies, waits for them, and re-layouts  37.1 us (6%)
  other arithmetic  21.1 us (4%)
  between operations  13.4 us (2%)
  starting transfers between devices  8.37 us (1%)
    all_to_all x2, blocking collectives, sum_at_owner(): tiles = lax.all_to_all(cut_along(x, dim, devices), axis, 0, 0, tiled=True)  88.6 us
    all_to_all x1, blocking collectives, track_windows(): lax.all_to_all(jnp.stack([z_in for _ in range(lax.axis_size(group_axis))]...  88.4 us
    reduce_scatter x1, waiting for transfers between devices, local(): lax.psum_scatter(jnp.dot(picked, weight_flat, preferred_element_type=jnp....  82.4 us
    reduce_scatter x2, waiting for transfers between devices, sum_by_axis(): nearer = lax.psum_scatter(x, axes[0], scatter_dimension=dim, tiled=True)  67.5 us
    all_to_all x2, blocking collectives, from_everyone(): return lax.all_to_all(copies, axis, split_axis=0, concat_axis=0, tiled=True)  45 us
    all_gather x1, waiting for transfers between devices, local(): gathered = lax.all_gather(blocks, TP, axis=0, tiled=True)  39.4 us
    all_to_all x1, waiting for transfers between devices, from_everyone(): return lax.all_to_all(copies, axis, split_axis=0, concat_axis=0, tiled=True)  36.8 us
    dot_general x1, matrix products, local(): jnp.dot(picked, weight_flat, preferred_element_type=jnp.float32)  22.3 us
  transfers between devices with their start and end apart: 5, of which 5 were waited for; matrix products, arithmetic and copies ran while one was open for 2% of the time, Pallas kernels for 0%

profile of v1, /device:TPU:0, one launch (start us, length us, event | category | flops | bytes accessed | tf_op | source)
XLA Modules:
  0.0 596.4 jit_solution(11052768886036411921)
XLA Ops:
  6.5 1.2 convert_reduce_fusion.1
  7.7 1.1 fusion.11
  8.9 1.0 fusion.13
  9.9 1.8 broadcast_in_dim.26
  11.7 8.2 %all-to-all-start = ((bf16[16,64,1280]{2,1,0:T(8,128)(2,1)}), bf16[16,64,1280]{2,1,0:T(8,128)(2,1)}, u32[]{:S(2)}, u32[]{:S(2)}) async-start(bf16[16,64,1280]{2,1,0:T(8,128)(2,1)} %broadcast_in_dim.26), calls=%async_computation | async-start | bytes 5242880 | tf_op jit(solution)/shard_map/all_to_all | solution.py:28
  19.9 0.0 all-gather.2.cloned.1.call-start
  20.0 0.2 reduce-window.8
  20.2 0.1 fusion.57
  20.3 36.8 %all-to-all-done = bf16[16,64,1280]{2,1,0:T(8,128)(2,1)} async-done(((bf16[16,64,1280]{2,1,0:T(8,128)(2,1)}), bf16[16,64,1280]{2,1,0:T(8,128)(2,1)}, u32[]{:S(2)}, u32[]{:S(2)}) %all-to-all-start) | async-done | bytes 2621472 | tf_op jit(solution)/shard_map/all_to_all | solution.py:28
  57.1 2.7 convolution_convert_fusion.4
  59.8 0.9 fusion.4
  60.7 1.9 copy-done.3
  62.6 1.0 fusion.3
  63.6 6.0 %convolution_convert_fusion.2 = bf16[1024,1280]{1,0:T(8,128)(2,1)} fusion(bf16[80,1280]{1,0:T(8,128)(2,1)S(1)} %copy-done.6, f32[1024,1024]{0,1:T(8,128)} %copy-done.3, f32[1024]{0:T(1024)S(1)} %fusion.3, f32[1024]{0:T(1024)S(1)} %get-tuple-element.5, s32[1024]{0:T(1024)S(1)} %fusion.57, bf16[1024,3,1,80]{0,3,1,2:T(8,128)(2,1)} %bitcast.68), kind=kOutput, calls=%fused_computation.14 | convolution fusion | flops 385171456 | bytes 7200768 | tf_op jit(solution)/shard_map/dot_general | solution.py:129
  69.6 37.0 %all_to_all.50 = bf16[16,64,1280]{2,1,0:T(8,128)(2,1)S(1)} all-to-all(bf16[16,64,1280]{2,1,0:T(8,128)(2,1)} %bitcast.59), channel_id=1, replica_groups=mesh['seq'=8,'tp_0'=4,'tp_1'=4] {'tp_0','tp_1'}, dimensions={0} | all-to-all | bytes 5242880 | tf_op jit(solution)/shard_map/all_to_all | solution.py:49
  106.6 0.4 convert_reduce_fusion
  107.0 0.1 fusion.56
  107.1 0.2 multiply_reduce_fusion.1
  107.4 0.1 multiply_convert_fusion.2
  107.5 0.8 reshape.153
  108.3 1.2 broadcast_in_dim.47
  109.5 35.3 %all_to_all.51 = bf16[16,16,5120]{2,1,0:T(8,128)(2,1)} all-to-all(bf16[16,16,5120]{2,1,0:T(8,128)(2,1)S(1)} %broadcast_in_dim.47), channel_id=1, replica_groups=mesh['seq'=8,'tp_0'=4,'tp_1'=4] {'tp_0','tp_1'}, dimensions={0} | all-to-all | bytes 5242880 | tf_op jit(solution)/shard_map/all_to_all | solution.py:28
  144.8 10.9 %convolution_convert_fusion.1 = bf16[256,8192]{1,0:T(8,128)(2,1)} fusion(bf16[320,8192]{1,0:T(8,128)(2,1)} %param.20, bf16[256,5120]{1,0:T(8,128)(2,1)} %bitcast.60, bf16[5120,320]{0,1:T(8,128)(2,1)S(1)} %copy-done), kind=kOutput, calls=%fused_computation.3 | convolution fusion | flops 2188460032 | bytes 15335424 | tf_op jit(solution)/shard_map/dot_general | solution.py:144
  155.7 51.6 %all_to_all.52 = bf16[16,16,8192]{2,1,0:T(8,128)(2,1)} all-to-all(bf16[16,16,8192]{2,1,0:T(8,128)(2,1)} %bitcast.58), channel_id=1, replica_groups=mesh['seq'=8,'tp_0'=4,'tp_1'=4] {'tp_0','tp_1'}, dimensions={0} | all-to-all | bytes 8388608 | tf_op jit(solution)/shard_map/all_to_all | solution.py:49
  207.3 2.9 reduce_sum.100
  210.2 11.7 %all_to_all.53 = bf16[16,8,1024]{2,0,1:T(8,128)(2,1)} all-to-all(bf16[16,8,1024]{2,0,1:T(8,128)(2,1)S(1)} %bitcast.63), channel_id=1, replica_groups=mesh['seq'=8,'tp_0'=4,'tp_1'=4] {'seq'}, dimensions={1} | all-to-all | bytes 524288 | tf_op jit(solution)/shard_map/all_to_all | solution.py:146
  222.0 0.0 reduce-scatter.4.cloned.1.call-start
  222.0 8.0 %scatter_custom_fusion = s32[2048]{0:T(1024)S(1)} fusion(s32[2048]{0:T(1024)S(1)} %compare_select_fusion.1, s32[2048]{0:T(1024)S(1)} %iota.7, s32[]{:T(128)} %constant.45.clone.1), kind=kCustom, calls=%fused_computation.97 | custom fusion | bytes 8196 | tf_op jit(solution)/shard_map/scatter | solution.py:93
  230.1 39.4 %all-gather.2.cloned.1.call-done = bf16[2048,1024]{1,0:T(8,128)(2,1)} async-done(((bf16[128,1024]{1,0:T(8,128)(2,1)}), bf16[2048,1024]{1,0:T(8,128)(2,1)}) %all-gather.2.cloned.1.call-update) | async-done | bytes 4194320 | tf_op jit(solution)/shard_map/all_gather | solution.py:147
  269.6 5.0 copy.28
  274.6 13.7 %gather_fusion = bf16[2048,1024]{1,0:T(8,128)(2,1)} fusion(bf16[2048,1024]{1,0:T(8,128)(2,1)} %bitcast.54, s32[2048]{0:T(1024)S(1)} %fusion.58), kind=kCustom, calls=%fused_computation | custom fusion | bytes 8396800 | tf_op jit(solution)/shard_map/jit(_take)/gather | solution.py:155
  288.2 3.1 multiply_reduce_fusion
  291.4 9.7 %all_to_all.54 = f32[8,1,2048]{2,1,0:T(1,128)S(1)} all-to-all(f32[8,1,2048]{2,1,0:T(1,128)S(1)} %broadcast_in_dim.50), channel_id=1, replica_groups=mesh['seq'=8,'tp_0'=4,'tp_1'=4] {'seq'}, dimensions={0} | all-to-all | bytes 131072 | tf_op jit(solution)/shard_map/all_to_all | solution.py:28
  301.1 0.1 reduce_sum.102
  301.1 22.3 %convolution_convert_fusion = bf16[2048,3696]{0,1:T(8,128)(2,1)} fusion(bf16[1024,3696]{0,1:T(8,128)(2,1)} %bitcast.64, f32[1024]{0:T(1024)S(1)} %copy-done.7, f32[2048]{0:T(1024)S(1)} %add_rsqrt_fusion, bf16[2048,1024]{1,0:T(8,128)(2,1)} %gather_fusion, pred[2048]{0:T(1024)(128)(4,1)S(1)} %compare_and_fusion), kind=kOutput, calls=%fused_computation.2 | convolution fusion | flops 15520202752 | bytes 26916864 | tf_op jit(solution)/shard_map/dot_general | solution.py:166
  323.5 0.0 reduce-scatter.6.cloned.1.call-start
  323.5 82.4 %reduce-scatter.4.cloned.1.call-done = bf16[256,3696]{0,1:T(8,128)(2,1)} async-done(((bf16[2048,3696]{0,1:T(8,128)(2,1)}), bf16[256,3696]{0,1:T(8,128)(2,1)}) %reduce-scatter.4.cloned.1.call-update) | async-done | bytes 1892368 | tf_op jit(solution)/shard_map/reduce_scatter | solution.py:165
  405.9 1.8 convert_element_type.83
  407.7 0.6 fusion.6
  408.3 0.5 stack.2
  408.8 88.4 %all_to_all.55 = bf16[8,256,1848]{1,2,0:T(8,128)(2,1)S(1)} all-to-all(bf16[8,256,1848]{1,2,0:T(8,128)(2,1)S(1)} %stack.2), channel_id=1, replica_groups=mesh['seq'=8,'tp_0'=4,'tp_1'=4] {'seq'}, dimensions={0} | all-to-all | bytes 15138816 | tf_op jit(solution)/shard_map/all_to_all | solution.py:16
  497.2 4.1 copy.33
  501.3 13.7 %convolution_convert_fusion.3 = bf16[2048,1024]{1,0:T(8,128)(2,1)} fusion(bf16[2048,1848]{0,1:T(8,128)(2,1)} %bitcast.56, bf16[1848,1024]{1,0:T(8,128)(2,1)} %param.23), kind=kOutput, calls=%fused_computation.15 | convolution fusion | flops 7753170944 | bytes 15548416 | tf_op jit(solution)/shard_map/dot_general | solution.py:174
  515.1 0.0 reduce-scatter.8.cloned.1.call-start
  515.1 46.8 %reduce-scatter.6.cloned.1.call-done = bf16[512,1024]{1,0:T(8,128)(2,1)} async-done(((bf16[2048,1024]{1,0:T(8,128)(2,1)}), bf16[512,1024]{1,0:T(8,128)(2,1)}) %reduce-scatter.6.cloned.1.call-update) | async-done | bytes 1048592 | tf_op jit(solution)/shard_map/reduce_scatter | solution.py:61
  562.0 5.3 fusion.95
  567.3 20.7 %reduce-scatter.8.cloned.1.call-done = bf16[128,1024]{1,0:T(8,128)(2,1)} async-done(((bf16[512,1024]{1,0:T(8,128)(2,1)}), bf16[128,1024]{1,0:T(8,128)(2,1)}) %reduce-scatter.8.cloned.1.call-update) | async-done | bytes 262160 | tf_op jit(solution)/shard_map/reduce_scatter | solution.py:61
  588.0 1.9 add_convert_fusion
  (35 shorter events, 0.2 us)
Async XLA Ops:
  6.5 138.2 %copy-start = (bf16[5120,320]{0,1:T(8,128)(2,1)S(1)}, bf16[5120,320]{0,1:T(8,128)(2,1)}, u32[]{:S(2)}) copy-start(bf16[5120,320]{0,1:T(8,128)(2,1)} %param.19) | copy-start | bytes 9830404
  8.9 11.1 %copy-start.8 = (s32[1,2]{1,0:T(1,128)S(1)}, s32[1,2]{1,0:T(1,128)}, u32[]{:S(2)}) copy-start(s32[1,2]{1,0:T(1,128)} %param.13) | copy-start | bytes 28
  11.7 45.3 %all-to-all-start = ((bf16[16,64,1280]{2,1,0:T(8,128)(2,1)}), bf16[16,64,1280]{2,1,0:T(8,128)(2,1)}, u32[]{:S(2)}, u32[]{:S(2)}) async-start(bf16[16,64,1280]{2,1,0:T(8,128)(2,1)} %broadcast_in_dim.26), calls=%async_computation | async-start | bytes 5242880 | tf_op jit(solution)/shard_map/all_to_all | solution.py:28
  19.9 249.6 %all-gather.2.cloned.1.call-start = ((), (), s32[]{:S(2)}) async-start(), calls=%async_computation.10 | async-start | bytes 4456448 | tf_op jit(solution)/shard_map/all_gather | solution.py:147
  59.8 0.9 copy-start.9
  59.8 3.8 copy-start.6
  60.7 1.9 copy-start.3
  69.6 37.4 %copy-start.2 = (bf16[64,1280]{1,0:T(8,128)(2,1)S(1)}, bf16[64,1280]{1,0:T(8,128)(2,1)}, u32[]{:S(2)}) copy-start(bf16[64,1280]{1,0:T(8,128)(2,1)} %param.12) | copy-start | bytes 491524
  69.6 37.7 %copy-start.5 = (f32[1280]{0:T(1024)S(1)}, f32[1280]{0:T(1024)}, u32[]{:S(2)}) copy-start(f32[1280]{0:T(1024)} %param.18) | copy-start | bytes 15364
  207.3 14.7 %copy-start.4 = (s32[2048]{0:T(1024)S(1)}, s32[2048]{0:T(1024)}, u32[]{:S(2)}) copy-start(s32[2048]{0:T(1024)} %param.14) | copy-start | bytes 24580
  222.0 184.0 %reduce-scatter.4.cloned.1.call-start = ((), (), s32[]{:S(2)}) async-start(), calls=%async_computation.11 | async-start | bytes 17031168 | tf_op jit(solution)/shard_map/reduce_scatter | solution.py:165
  288.2 12.9 %copy-start.7 = (f32[1024]{0:T(1024)S(1)}, f32[1024]{0:T(1024)}, u32[]{:S(2)}) copy-start(f32[1024]{0:T(1024)} %param.21) | copy-start | bytes 12292
  323.5 238.4 %reduce-scatter.6.cloned.1.call-start = ((), (), s32[]{:S(2)}) async-start(), calls=%async_computation.12 | async-start | bytes 5242880 | tf_op jit(solution)/shard_map/reduce_scatter | solution.py:61
  515.1 72.9 %reduce-scatter.8.cloned.1.call-start = ((), (), s32[]{:S(2)}) async-start(), calls=%async_computation.13 | async-start | bytes 1310720 | tf_op jit(solution)/shard_map/reduce_scatter | solution.py:61
  562.0 27.9 %copy-start.1 = (bf16[5120,320]{0,1:T(8,128)(2,1)S(1)}, bf16[5120,320]{0,1:T(8,128)(2,1)}, u32[]{:S(2)}) copy-start(bf16[5120,320]{0,1:T(8,128)(2,1)} %param.19) | copy-start | bytes 9830404
Sparse Core Ops, SparseCore 0:
  222.1 47.4 all-gather.1
  323.6 82.2 reduce-scatter.3
  515.2 46.7 reduce-scatter.5
  564.2 23.7 reduce-scatter.7
